TPU v7x, 32 devices: a whole 2x2x4 slice. The times are simulated.
32 devices in a mesh: dp: 8 (over y, x, core), tensor: 4 (over z).
Axes of the slice: x: 2, y: 2, z: 4, core: 2. Of those that a mesh axis runs over, the one named last changes fastest.
Arguments:
- tokens: bfloat16 [16, 320, 1536], P('dp', 'tensor'), may hold values from -6 to 6
- cotangent: bfloat16 [16, 320, 1536], P('dp', 'tensor'), may hold values from -6 to 6
- order: int32 [16, 320], P('dp'), may hold values from 0 to 319, each once within a row
- lengths: int32 [16, 3], P('dp'), may hold values from 1 to 256, 320 in all within a row
- gain_attn: bfloat16 [1536], P('dp'), may hold values from 0.5 to 1.5
- w_query: bfloat16 [1536, 1536], P('dp', 'tensor'), may hold values from -0.15625 to 0.15625
- w_key: bfloat16 [1536, 768], P('dp', 'tensor'), may hold values from -0.15625 to 0.15625
- w_value: bfloat16 [1536, 768], P('dp', 'tensor'), may hold values from -0.15625 to 0.15625
- w_out: bfloat16 [1536, 1536], P('tensor', 'dp'), may hold values from -1.5 to 1.5
- gain_ffn: bfloat16 [1536], P('dp'), may hold values from 0.5 to 1.5
- w_gate: bfloat16 [1536, 4096], P('dp', 'tensor'), may hold values from -0.15625 to 0.15625
- w_up: bfloat16 [1536, 4096], P('dp', 'tensor'), may hold values from -0.15625 to 0.15625
- w_down: bfloat16 [4096, 1536], P('tensor', 'dp'), may hold values from -0.09375 to 0.09375
Outputs:
- output: bfloat16 [16, 320, 1536], P('dp', 'tensor')
- grad_tokens: float32 [16, 320, 1536], P('dp', 'tensor')
- grad_gain_attn: float32 [1536], P('dp')
- grad_query: float32 [1536, 1536], P('dp', 'tensor')
- grad_key: float32 [1536, 768], P('dp', 'tensor')
- grad_value: float32 [1536, 768], P('dp', 'tensor')
- grad_out: float32 [1536, 1536], P('tensor', 'dp')
- grad_gain_ffn: float32 [1536], P('dp')
- grad_gate: float32 [1536, 4096], P('dp', 'tensor')
- grad_up: float32 [1536, 4096], P('dp', 'tensor')
- grad_down: float32 [4096, 1536], P('tensor', 'dp')
Inputs may be any that keep to these rules, and one draw needn't show every extreme that they name: `order`: each row is a permutation of 0 to 319. `lengths`: each row sums to 320; its largest entry is 256; the last document of each stream is padding.
All inputs are finite; a program needn't handle non-finite values.
Results may differ from a plain program's by a relative error of at most 0.012.
Values may be sent and summed in bfloat16 or wider, within the bound.
A program may use at most 128 MiB of HBM per device.

v0:
```python
import jax
import jax.numpy as jnp
from jax import lax
from jax.sharding import PartitionSpec as P

HEAD = 96
eps = 1e-05
rope_base = 100000.0


def rotate(field, cosine, sine):
    half = field.shape[-1] // 2
    first = field[..., :half]
    second = field[..., half:]
    return jnp.concatenate(
        [first * cosine - second * sine, second * cosine + first * sine], axis=-1
    )


def rotate_back(field, cosine, sine):
    half = field.shape[-1] // 2
    first = field[..., :half]
    second = field[..., half:]
    return jnp.concatenate(
        [first * cosine + second * sine, second * cosine - first * sine], axis=-1
    )


def layout(order, lengths):
    starts = jnp.cumsum(lengths, dtype=jnp.int32) - lengths
    docs = jnp.sum((order[:, None] >= starts[None, 1:]).astype(jnp.int32), axis=1, dtype=jnp.int32)
    onehot = docs[:, None] == jnp.arange(lengths.shape[0], dtype=jnp.int32)[None, :]
    first = jnp.sum(jnp.where(onehot, starts[None, :], 0), axis=1, dtype=jnp.int32)
    positions = (order - first).astype(jnp.float32)
    mask = (docs[:, None] == docs[None, :]) & (order[None, :] <= order[:, None])
    real = (docs < lengths.shape[0] - 1).astype(jnp.float32)
    return (positions, mask, real)


def norm_forward(rows, gain):
    scale = lax.rsqrt(jnp.mean(rows * rows, axis=-1, keepdims=True) + eps)
    unit = rows * scale
    return (unit, scale, (unit * gain).astype(jnp.bfloat16))


def norm_backward(grad, unit, scale, gain):
    inner = grad * gain
    return scale * (inner - unit * jnp.mean(inner * unit, axis=-1, keepdims=True))


def contract_rows(left, right):
    return lax.dot_general(
        left, right, (((0,), (0,)), ((), ())), preferred_element_type=jnp.float32
    )


def times_transpose(left, right):
    return lax.dot_general(
        left, right, (((1,), (1,)), ((), ())), preferred_element_type=jnp.float32
    )


def gather_weights(gain_attn, w_query, w_key, w_value, w_out, gain_ffn, w_gate, w_up, w_down):
    gains = lax.all_gather(jnp.stack([gain_attn, gain_ffn], axis=0), "dp", axis=1, tiled=True)
    attn = lax.all_gather(
        jnp.concatenate([w_query, w_key, w_value, w_out.T], axis=1), "dp", axis=0, tiled=True
    )
    gate_up = lax.all_gather(jnp.concatenate([w_gate, w_up], axis=1), "dp", axis=0, tiled=True)
    down = lax.all_gather(w_down.T, "dp", axis=0, tiled=True)
    return (gains, attn, gate_up, down)


def gather_rows(rows):
    return lax.all_gather(rows, "tensor", axis=1, tiled=True)


def scatter_rows(partial):
    low = partial.astype(jnp.bfloat16)
    return lax.psum_scatter(low, "tensor", scatter_dimension=1, tiled=True).astype(jnp.float32)


def reduce_weights(term):
    low = term.astype(jnp.bfloat16)
    return lax.psum_scatter(low, "dp", scatter_dimension=0, tiled=True).astype(jnp.float32)


def local(
    tokens,
    cotangent,
    order,
    lengths,
    gain_attn,
    w_query,
    w_key,
    w_value,
    w_out,
    gain_ffn,
    w_gate,
    w_up,
    w_down,
):
    micro, rows, width = tokens.shape
    seq = rows * lax.axis_size("tensor")
    q_cols, k_cols, ff_cols = (w_query.shape[1], w_key.shape[1], w_gate.shape[1])
    local_heads, local_kv = (q_cols // HEAD, k_cols // HEAD)
    group = local_heads // local_kv
    first_row = lax.axis_index("tensor") * rows
    freqs = rope_base ** (-2.0 * jnp.arange(HEAD // 2, dtype=jnp.float32) / HEAD)
    head_scale = HEAD ** (-0.5)
    gains, attn, gate_up, down = gather_weights(
        gain_attn, w_query, w_key, w_value, w_out, gain_ffn, w_gate, w_up, w_down
    )
    gain1, gain2 = (gains[0].astype(jnp.float32), gains[1].astype(jnp.float32))
    in_cols = q_cols + 2 * k_cols
    w_in, w_out_t = (attn[:, :in_cols], attn[:, in_cols:])
    positions, mask, real = jax.vmap(layout)(order, lengths)
    angles = positions[:, :, None] * freqs
    cosine, sine = (jnp.cos(angles)[:, :, None, :], jnp.sin(angles)[:, :, None, :])
    mask = mask[:, None, None]
    real_rows = lax.dynamic_slice_in_dim(real, first_row, rows, 1)[:, :, None]
    stream = tokens.astype(jnp.float32)
    unit1, scale1, normed1 = norm_forward(stream, gain1)
    full1 = gather_rows(normed1)
    grad_out_rows = cotangent.astype(jnp.float32) * real_rows
    full_grad = gather_rows(grad_out_rows.astype(jnp.bfloat16))
    flat1 = full1.reshape(micro * seq, width)
    flat_grad = full_grad.reshape(micro * seq, width)
    mixed_in = jnp.dot(flat1, w_in, preferred_element_type=jnp.float32).reshape(micro, seq, in_cols)
    query = mixed_in[..., :q_cols].reshape(micro, seq, local_heads, HEAD)
    keys = mixed_in[..., q_cols : q_cols + k_cols].reshape(micro, seq, local_kv, HEAD)
    values = (
        mixed_in[..., q_cols + k_cols :].reshape(micro, seq, local_kv, HEAD).astype(jnp.bfloat16)
    )
    query = (rotate(query, cosine, sine) * head_scale).astype(jnp.bfloat16)
    query = query.reshape(micro, seq, local_kv, group, HEAD)
    keys = rotate(keys, cosine, sine).astype(jnp.bfloat16)
    scores = jnp.einsum("bqkgd,bskd->bkgqs", query, keys, preferred_element_type=jnp.float32)
    scores = jnp.where(mask, scores, -1e30)
    peak = jnp.max(scores, axis=-1, keepdims=True)
    expon = jnp.exp(scores - peak)
    total = jnp.sum(expon, axis=-1, keepdims=True)
    probs = expon / total
    probs_low = probs.astype(jnp.bfloat16)
    mixed = jnp.einsum("bkgqs,bskd->bqkgd", probs_low, values, preferred_element_type=jnp.float32)
    mixed = mixed.reshape(micro * seq, q_cols).astype(jnp.bfloat16)
    branch = scatter_rows(times_transpose(mixed, w_out_t).reshape(micro, seq, width))
    resid = stream + branch
    unit2, scale2, normed2 = norm_forward(resid, gain2)
    full2 = gather_rows(normed2).reshape(micro * seq, width)
    both = jnp.dot(full2, gate_up, preferred_element_type=jnp.float32)
    gate, upper = (both[:, :ff_cols], both[:, ff_cols:])
    sigma = jax.nn.sigmoid(gate)
    hidden = (gate * sigma * upper).astype(jnp.bfloat16)
    ffn = scatter_rows(times_transpose(hidden, down).reshape(micro, seq, width))
    output = ((resid + ffn) * real_rows).astype(jnp.bfloat16)
    grad_hidden = jnp.dot(flat_grad, down, preferred_element_type=jnp.float32)
    grad_gate = (grad_hidden * upper * sigma * (1.0 + gate * (1.0 - sigma))).astype(jnp.bfloat16)
    grad_up = (grad_hidden * gate * sigma).astype(jnp.bfloat16)
    grad_both = jnp.concatenate([grad_gate, grad_up], axis=1)
    grad_norm2 = scatter_rows(times_transpose(grad_both, gate_up).reshape(micro, seq, width))
    final_down = reduce_weights(contract_rows(flat_grad, hidden))
    final_gate = reduce_weights(contract_rows(full2, grad_gate))
    final_up = reduce_weights(contract_rows(full2, grad_up))
    term_gain2 = jnp.sum(grad_norm2 * unit2, axis=(0, 1))
    grad_resid = grad_out_rows + norm_backward(grad_norm2, unit2, scale2, gain2)
    full_resid = gather_rows(grad_resid.astype(jnp.bfloat16)).reshape(micro * seq, width)
    grad_mixed = jnp.dot(full_resid, w_out_t, preferred_element_type=jnp.float32).astype(
        jnp.bfloat16
    )
    final_out = reduce_weights(contract_rows(full_resid, mixed))
    grad_heads = grad_mixed.reshape(micro, seq, local_kv, group, HEAD)
    grad_probs = jnp.einsum(
        "bqkgd,bskd->bkgqs", grad_heads, values, preferred_element_type=jnp.float32
    )
    grad_values = jnp.einsum(
        "bkgqs,bqkgd->bskd", probs_low, grad_heads, preferred_element_type=jnp.float32
    )
    grad_scores = (
        probs * (grad_probs - jnp.sum(probs * grad_probs, axis=-1, keepdims=True))
    ).astype(jnp.bfloat16)
    grad_query = jnp.einsum(
        "bkgqs,bskd->bqkgd", grad_scores, keys, preferred_element_type=jnp.float32
    ).reshape(micro, seq, local_heads, HEAD)
    grad_keys = jnp.einsum(
        "bkgqs,bqkgd->bskd", grad_scores, query, preferred_element_type=jnp.float32
    )
    grad_query = rotate_back(grad_query * head_scale, cosine, sine).reshape(micro * seq, q_cols)
    grad_keys = rotate_back(grad_keys, cosine, sine).reshape(micro * seq, k_cols)
    grad_values = grad_values.reshape(micro * seq, k_cols)
    grad_in = jnp.concatenate(
        [
            grad_query.astype(jnp.bfloat16),
            grad_keys.astype(jnp.bfloat16),
            grad_values.astype(jnp.bfloat16),
        ],
        axis=1,
    )
    grad_norm1 = scatter_rows(times_transpose(grad_in, w_in).reshape(micro, seq, width))
    final_in = reduce_weights(contract_rows(flat1, grad_in))
    term_gain1 = jnp.sum(grad_norm1 * unit1, axis=(0, 1))
    grad_tokens = grad_resid + norm_backward(grad_norm1, unit1, scale1, gain1)
    gain_terms = lax.psum(jnp.stack([term_gain1, term_gain2], axis=0), ("dp", "tensor"))
    own = gain_attn.shape[0]
    gain_own = lax.dynamic_slice_in_dim(gain_terms, lax.axis_index("dp") * own, own, 1)
    return (
        output,
        grad_tokens,
        gain_own[0],
        final_in[:, :q_cols],
        final_in[:, q_cols : q_cols + k_cols],
        final_in[:, q_cols + k_cols :],
        final_out.T,
        gain_own[1],
        final_gate,
        final_up,
        final_down.T,
    )


def solution(mesh):
    return jax.shard_map(
        local,
        mesh=mesh,
        in_specs=(
            P("dp", "tensor", None),
            P("dp", "tensor", None),
            P("dp", None),
            P("dp", None),
            P("dp"),
            P("dp", "tensor"),
            P("dp", "tensor"),
            P("dp", "tensor"),
            P("tensor", "dp"),
            P("dp"),
            P("dp", "tensor"),
            P("dp", "tensor"),
            P("tensor", "dp"),
        ),
        out_specs=(
            P("dp", "tensor", None),
            P("dp", "tensor", None),
            P("dp"),
            P("dp", "tensor"),
            P("dp", "tensor"),
            P("dp", "tensor"),
            P("tensor", "dp"),
            P("dp"),
            P("dp", "tensor"),
            P("dp", "tensor"),
            P("tensor", "dp"),
        ),
        check_vma=False,
    )
```

profile of v0, /device:TPU:0, one launch (start us, length us, event | category | flops | bytes accessed | tf_op | source)
XLA Modules:
  0.0 763.6 jit_solution(17415708524543095408)
XLA Ops:
  7.3 0.8 stack.18
  8.8 1.2 fusion.38
  10.0 10.4 %all-gather = bf16[8,192,2]{1,2,0:T(2,128)(2,1)S(1)} all-gather(bf16[1,192,2]{1,2,0:T(2,128)(2,1)S(1)} %maximum_bitcast_fusion.8), channel_id=1, replica_groups=mesh['dp'=8,'tensor'=4] {'dp'}, dimensions={0}, use_global_device_ids=true | all-gather | bytes 6912 | tf_op jit(solution)/shard_map/all_gather | solution.py:64
  20.6 2.0 fusion.35
  22.7 0.9 concatenate.32
  24.2 1.0 compare_and_fusion
  25.8 40.8 %all-gather.9.cloned.1.call-done = bf16[2,320,1536]{2,1,0:T(8,128)(2,1)} async-done(((bf16[2,80,1536]{2,1,0:T(8,128)(2,1)}), bf16[2,320,1536]{2,1,0:T(8,128)(2,1)}) %all-gather.9.cloned.1.call-update) | async-done | bytes 1966096 | tf_op jit(solution)/shard_map/all_gather | solution.py:74
  66.5 35.2 %all-gather.11.cloned.1.call-done = bf16[1536,1152]{1,0:T(8,128)(2,1)} async-done(((bf16[192,1152]{1,0:T(8,128)(2,1)}), bf16[1536,1152]{1,0:T(8,128)(2,1)}) %all-gather.11.cloned.1.call-update) | async-done | bytes 3538960 | tf_op jit(solution)/shard_map/all_gather | solution.py:65
  101.7 3.9 fusion.8
  105.9 0.9 copy.89
  107.7 4.7 fusion.63
  112.5 2.7 convolution_convert_fusion.9
  115.2 3.9 convolution_convert_fusion.7
  119.2 0.9 pad_maximum_fusion
  120.3 40.7 %reduce-scatter.10.cloned.1.call-done = bf16[2,80,1536]{2,1,0:T(8,128)(2,1)} async-done(((bf16[2,320,1536]{2,1,0:T(8,128)(2,1)}), bf16[2,80,1536]{2,1,0:T(8,128)(2,1)}) %reduce-scatter.10.cloned.1.call-update) | async-done | bytes 491536 | tf_op jit(solution)/shard_map/reduce_scatter | solution.py:79
  160.9 1.3 multiply_reduce_fusion
  162.2 2.0 multiply_convert_fusion.4
  164.4 0.9 fusion.39
  166.6 41.2 %all-gather.15.cloned.1.call-done = bf16[1536,2048]{1,0:T(8,128)(2,1)} async-done(((bf16[192,2048]{1,0:T(8,128)(2,1)}), bf16[1536,2048]{1,0:T(8,128)(2,1)}) %all-gather.15.cloned.1.call-update) | async-done | bytes 6291472 | tf_op jit(solution)/shard_map/all_gather | solution.py:68
  207.8 45.5 %all-gather.13.cloned.1.call-done = bf16[2,320,1536]{2,1,0:T(8,128)(2,1)} async-done(((bf16[2,80,1536]{2,1,0:T(8,128)(2,1)}), bf16[2,320,1536]{2,1,0:T(8,128)(2,1)}) %all-gather.13.cloned.1.call-update) | async-done | bytes 1966096 | tf_op jit(solution)/shard_map/all_gather | solution.py:74
  253.3 10.0 %fusion.68 = f32[640,2048]{1,0:T(8,128)} fusion(bf16[640,1536]{1,0:T(8,128)(2,1)} %bitcast.147, bf16[1536,2048]{1,0:T(8,128)(2,1)} %all-gather.15.cloned.1.call-done), kind=kOutput, calls=%fused_computation.125 | convolution fusion | flops 4026531840 | bytes 13500416 | tf_op jit(solution)/shard_map/dot_general | solution.py:150
  263.3 34.4 %all-gather.19.cloned.1.call-done = bf16[2,320,1536]{2,1,0:T(8,128)(2,1)} async-done(((bf16[2,80,1536]{2,1,0:T(8,128)(2,1)}), bf16[2,320,1536]{2,1,0:T(8,128)(2,1)}) %all-gather.19.cloned.1.call-update) | async-done | bytes 1966096 | tf_op jit(solution)/shard_map/all_gather | solution.py:74
  297.6 32.9 %all-gather.17.cloned.1.call-done = bf16[1536,1024]{1,0:T(8,128)(2,1)} async-done(((bf16[192,1024]{1,0:T(8,128)(2,1)}), bf16[1536,1024]{1,0:T(8,128)(2,1)}) %all-gather.17.cloned.1.call-update) | async-done | bytes 3145744 | tf_op jit(solution)/shard_map/all_gather | solution.py:69
  330.6 8.4 %multiply_convert_fusion.1 = (bf16[640,1024]{1,0:T(8,128)(2,1)S(1)}, bf16[640,1024]{1,0:T(8,128)(2,1)S(1)}, bf16[640,1024]{1,0:T(8,128)(2,1)}) fusion(f32[640,2048]{1,0:T(8,128)} %fusion.68, bf16[640,1536]{1,0:T(8,128)(2,1)} %bitcast.150, bf16[1536,1024]{1,0:T(8,128)(2,1)} %all-gather.17.cloned.1.call-done), kind=kOutput, calls=%fused_computation.22 | convolution fusion | flops 2023751680 | bytes 14286848 | tf_op jit(solution)/shard_map/dot_general | solution.py:156
  339.0 5.5 convolution_convert_fusion.5
  344.6 41.7 %reduce-scatter.14.cloned.1.call-done = bf16[2,80,1536]{2,1,0:T(8,128)(2,1)} async-done(((bf16[2,320,1536]{2,1,0:T(8,128)(2,1)}), bf16[2,80,1536]{2,1,0:T(8,128)(2,1)}) %reduce-scatter.14.cloned.1.call-update) | async-done | bytes 491536 | tf_op jit(solution)/shard_map/reduce_scatter | solution.py:79
  386.3 1.5 fusion.34
  387.8 2.2 fusion.43
  390.1 6.2 convolution_convert_fusion.2
  396.5 6.4 convolution_convert_fusion.1
  403.0 6.3 convolution_convert_fusion
  410.0 1.2 convert_element_type.210
  411.2 21.6 %all-gather.21.cloned.1.call-done = bf16[2,320,1536]{2,1,0:T(8,128)(2,1)} async-done(((bf16[2,80,1536]{2,1,0:T(8,128)(2,1)}), bf16[2,320,1536]{2,1,0:T(8,128)(2,1)}) %all-gather.21.cloned.1.call-update) | async-done | bytes 1966096 | tf_op jit(solution)/shard_map/all_gather | solution.py:74
  432.8 3.0 convolution_convert_fusion.10
  437.1 2.9 fusion.23
  440.3 0.9 convert_element_type.204
  441.2 3.3 fusion.1
  446.5 1.6 convolution_bitcast_fusion.1
  448.5 2.5 convolution_convert_fusion.8
  451.2 1.2 add_convert_fusion.1
  452.5 1.0 copy.100
  453.5 1.9 convert_element_type.201
  455.4 1.7 convolution_multiply_fusion
  458.6 0.9 copy-done.21
  460.3 3.4 convolution_convert_fusion.3
  463.8 1.2 copy-done.22
  465.0 4.8 convolution_convert_fusion.4
  469.8 1.2 copy-done.32
  471.0 5.4 convolution_convert_fusion.6
  476.5 4.5 reduce-scatter.22.cloned.1.call-done
  481.0 2.0 convert_element_type.213
  482.9 47.5 %reduce-scatter.24.cloned.1.call-done = bf16[192,1024]{1,0:T(8,128)(2,1)} async-done(((bf16[1536,1024]{1,0:T(8,128)(2,1)}), bf16[192,1024]{1,0:T(8,128)(2,1)}) %reduce-scatter.24.cloned.1.call-update) | async-done | bytes 393232 | tf_op jit(solution)/shard_map/reduce_scatter | solution.py:84
  530.5 2.0 convert_element_type.215
  532.4 47.4 %reduce-scatter.26.cloned.1.call-done = bf16[192,1024]{1,0:T(8,128)(2,1)} async-done(((bf16[1536,1024]{1,0:T(8,128)(2,1)}), bf16[192,1024]{1,0:T(8,128)(2,1)}) %reduce-scatter.26.cloned.1.call-update) | async-done | bytes 393232 | tf_op jit(solution)/shard_map/reduce_scatter | solution.py:84
  579.8 2.0 convert_bitcast_fusion
  581.8 38.0 %reduce-scatter.20.cloned.1.call-done = bf16[192,384]{1,0:T(8,128)(2,1)} async-done(((bf16[1536,384]{1,0:T(8,128)(2,1)}), bf16[192,384]{1,0:T(8,128)(2,1)}) %reduce-scatter.20.cloned.1.call-update) | async-done | bytes 147472 | tf_op jit(solution)/shard_map/reduce_scatter | solution.py:84
  619.7 1.6 convert_bitcast_fusion.1
  621.4 43.9 %reduce-scatter.18.cloned.1.call-done = bf16[192,768]{1,0:T(8,128)(2,1)} async-done(((bf16[1536,768]{1,0:T(8,128)(2,1)}), bf16[192,768]{1,0:T(8,128)(2,1)}) %reduce-scatter.18.cloned.1.call-update) | async-done | bytes 294928 | tf_op jit(solution)/shard_map/reduce_scatter | solution.py:84
  665.3 1.6 slice.110
  667.0 1.7 fusion.61
  668.7 40.4 %reduce-scatter.16.cloned.1.call-done = bf16[2,80,1536]{2,1,0:T(8,128)(2,1)} async-done(((bf16[2,320,1536]{2,1,0:T(8,128)(2,1)}), bf16[2,80,1536]{2,1,0:T(8,128)(2,1)}) %reduce-scatter.16.cloned.1.call-update) | async-done | bytes 491536 | tf_op jit(solution)/shard_map/reduce_scatter | solution.py:79
  709.1 1.4 fusion.37
  710.6 42.5 %psum.7 = f32[2,1536]{1,0:T(2,128)S(1)} all-reduce(f32[2,1536]{1,0:T(2,128)S(1)} %pad_maximum_fusion.3), channel_id=1, replica_groups=mesh['dp'=8,'tensor'=4] {'dp','tensor'}, use_global_device_ids=true, to_apply=%region_16.17 | all-reduce | flops 3072 | bytes 24576 | tf_op jit(solution)/shard_map/psum | solution.py:202
  753.7 3.1 fusion.30
  (143 shorter events, 13.1 us)
Async XLA Ops:
  7.2 15.5 %copy-start.24 = (bf16[384,192]{0,1:T(8,128)(2,1)S(1)}, bf16[384,192]{0,1:T(8,128)(2,1)}, u32[]{:S(2)}) copy-start(bf16[384,192]{0,1:T(8,128)(2,1)} %param.21) | copy-start | bytes 442372
  7.2 15.5 %copy-start.26 = (bf16[192,192]{1,0:T(8,128)(2,1)S(1)}, bf16[192,192]{1,0:T(8,128)(2,1)}, u32[]{:S(2)}) copy-start(bf16[192,192]{1,0:T(8,128)(2,1)} %param.20) | copy-start | bytes 221188
  7.2 15.5 %copy-start.25 = (bf16[192,192]{1,0:T(8,128)(2,1)S(1)}, bf16[192,192]{1,0:T(8,128)(2,1)}, u32[]{:S(2)}) copy-start(bf16[192,192]{1,0:T(8,128)(2,1)} %param.19) | copy-start | bytes 221188
  7.2 15.5 %copy-start.23 = (bf16[192,384]{1,0:T(8,128)(2,1)S(1)}, bf16[192,384]{1,0:T(8,128)(2,1)}, u32[]{:S(2)}) copy-start(bf16[192,384]{1,0:T(8,128)(2,1)} %param.18) | copy-start | bytes 442372
  7.2 16.4 %copy-start.28 = (s32[2,3]{1,0:T(2,128)S(1)}, s32[2,3]{1,0:T(2,128)}, u32[]{:S(2)}) copy-start(s32[2,3]{1,0:T(2,128)} %param.16) | copy-start | bytes 76
  7.2 16.8 %copy-start.27 = (s32[2,320]{1,0:T(2,128)S(1)}, s32[2,320]{1,0:T(2,128)}, u32[]{:S(2)}) copy-start(s32[2,320]{1,0:T(2,128)} %param.15) | copy-start | bytes 7684
  7.2 59.3 %all-gather.9.cloned.1.call-start = ((), (), s32[]{:S(2)}) async-start(), calls=%async_computation.9 | async-start | bytes 2457600 | tf_op jit(solution)/shard_map/all_gather | solution.py:74
  22.6 79.1 %all-gather.11.cloned.1.call-start = ((), (), s32[]{:S(2)}) async-start(), calls=%async_computation.10 | async-start | bytes 3981312 | tf_op jit(solution)/shard_map/all_gather | solution.py:65
  23.6 137.3 %reduce-scatter.10.cloned.1.call-start = ((), (), s32[]{:S(2)}) async-start(), calls=%async_computation.11 | async-start | bytes 2457600 | tf_op jit(solution)/shard_map/reduce_scatter | solution.py:79
  25.8 81.8 %copy-start.5 = (f32[2,320,48]{1,2,0:T(8,128)}, f32[2,320,48]{1,2,0:T(8,128)S(1)}, u32[]{:S(2)}) copy-start(f32[2,320,48]{1,2,0:T(8,128)S(1)} %get-tuple-element.34) | copy-start | bytes 368644
  25.8 81.8 %copy-start.7 = (f32[2,320,48]{1,2,0:T(8,128)}, f32[2,320,48]{1,2,0:T(8,128)S(1)}, u32[]{:S(2)}) copy-start(f32[2,320,48]{1,2,0:T(8,128)S(1)} %get-tuple-element.35) | copy-start | bytes 368644
  107.5 5.0 copy-start.15
  107.5 4.9 copy-start.16
  107.7 4.8 copy-start.9
  107.7 4.8 copy-start.11
  107.7 4.8 copy-start.20
  115.2 4.0 copy-start.18
  115.2 4.0 copy-start.19
  119.1 41.8 %copy-start = (bf16[2,80,1536]{2,1,0:T(8,128)(2,1)S(1)}, bf16[2,80,1536]{2,1,0:T(8,128)(2,1)}, u32[]{:S(2)}) copy-start(bf16[2,80,1536]{2,1,0:T(8,128)(2,1)} %param.13) | copy-start | bytes 1474564
  119.2 88.6 %all-gather.15.cloned.1.call-start = ((), (), s32[]{:S(2)}) async-start(), calls=%async_computation.13 | async-start | bytes 7077888 | tf_op jit(solution)/shard_map/all_gather | solution.py:68
  120.2 44.2 %copy-start.2 = (bf16[2,80,1536]{2,1,0:T(8,128)(2,1)S(1)}, bf16[2,80,1536]{2,1,0:T(8,128)(2,1)}, u32[]{:S(2)}) copy-start(bf16[2,80,1536]{2,1,0:T(8,128)(2,1)} %param.14) | copy-start | bytes 1474564
  120.2 133.1 %all-gather.13.cloned.1.call-start = ((), (), s32[]{:S(2)}) async-start(), calls=%async_computation.12 | async-start | bytes 2457600 | tf_op jit(solution)/shard_map/all_gather | solution.py:74
  164.2 133.4 %all-gather.19.cloned.1.call-start = ((), (), s32[]{:S(2)}) async-start(), calls=%async_computation.16 | async-start | bytes 2457600 | tf_op jit(solution)/shard_map/all_gather | solution.py:74
  165.3 165.3 %all-gather.17.cloned.1.call-start = ((), (), s32[]{:S(2)}) async-start(), calls=%async_computation.14 | async-start | bytes 3538944 | tf_op jit(solution)/shard_map/all_gather | solution.py:69
  166.1 220.2 %reduce-scatter.14.cloned.1.call-start = ((), (), s32[]{:S(2)}) async-start(), calls=%async_computation.17 | async-start | bytes 2457600 | tf_op jit(solution)/shard_map/reduce_scatter | solution.py:79
  330.6 8.4 %copy-start.29 = (bf16[1536,2048]{1,0:T(8,128)(2,1)S(1)}, bf16[1536,2048]{1,0:T(8,128)(2,1)}, u32[]{:S(2)}) copy-start(bf16[1536,2048]{1,0:T(8,128)(2,1)} %all-gather.15.cloned.1.call-done) | copy-start | bytes 18874372
  339.0 5.5 copy-start.33
  339.0 5.5 copy-start.34
  344.5 41.8 %copy-start.1 = (bf16[2,80,1536]{2,1,0:T(8,128)(2,1)S(1)}, bf16[2,80,1536]{2,1,0:T(8,128)(2,1)}, u32[]{:S(2)}) copy-start(bf16[2,80,1536]{2,1,0:T(8,128)(2,1)} %reduce-scatter.10.cloned.1.call-done) | copy-start | bytes 1474564
  344.5 88.3 %all-gather.21.cloned.1.call-start = ((), (), s32[]{:S(2)}) async-start(), calls=%async_computation.18 | async-start | bytes 2457600 | tf_op jit(solution)/shard_map/all_gather | solution.py:74
  390.0 90.9 %reduce-scatter.22.cloned.1.call-start = ((), (), s32[]{:S(2)}) async-start(), calls=%async_computation.22 | async-start | bytes 3538944 | tf_op jit(solution)/shard_map/reduce_scatter | solution.py:84
  396.3 134.2 %reduce-scatter.24.cloned.1.call-start = ((), (), s32[]{:S(2)}) async-start(), calls=%async_computation.23 | async-start | bytes 3538944 | tf_op jit(solution)/shard_map/reduce_scatter | solution.py:84
  402.9 176.9 %reduce-scatter.26.cloned.1.call-start = ((), (), s32[]{:S(2)}) async-start(), calls=%async_computation.24 | async-start | bytes 3538944 | tf_op jit(solution)/shard_map/reduce_scatter | solution.py:84
  409.3 210.4 %reduce-scatter.20.cloned.1.call-start = ((), (), s32[]{:S(2)}) async-start(), calls=%async_computation.21 | async-start | bytes 1327104 | tf_op jit(solution)/shard_map/reduce_scatter | solution.py:84
  441.2 3.9 copy-start.4
  445.1 1.1 copy-start.10
  445.1 1.3 copy-start.12
  446.5 1.6 copy-start.17
  446.5 2.0 copy-start.31
  451.0 214.3 %reduce-scatter.18.cloned.1.call-start = ((), (), s32[]{:S(2)}) async-start(), calls=%async_computation.20 | async-start | bytes 2654208 | tf_op jit(solution)/shard_map/reduce_scatter | solution.py:84
  455.4 1.7 copy-start.6
  455.4 1.7 copy-start.8
  457.2 1.2 copy-start.14
  457.3 1.2 copy-start.13
  458.4 1.9 copy-start.30
  458.5 0.9 copy-start.21
  463.7 1.2 copy-start.22
  463.8 245.3 %reduce-scatter.16.cloned.1.call-start = ((), (), s32[]{:S(2)}) async-start(), calls=%async_computation.19 | async-start | bytes 2457600 | tf_op jit(solution)/shard_map/reduce_scatter | solution.py:79
  469.7 1.3 copy-start.32
  469.8 284.0 %reduce-scatter.12.cloned.1.call-start = ((), (), s32[]{:S(2)}) async-start(), calls=%async_computation.15 | async-start | bytes 2457600 | tf_op jit(solution)/shard_map/reduce_scatter | solution.py:79
  532.4 221.3 %copy-start.3 = (bf16[2,80,1536]{2,1,0:T(8,128)(2,1)S(1)}, bf16[2,80,1536]{2,1,0:T(8,128)(2,1)}, u32[]{:S(2)}) copy-start(bf16[2,80,1536]{2,1,0:T(8,128)(2,1)} %reduce-scatter.14.cloned.1.call-done) | copy-start | bytes 1474564
Sparse Core Ops, SparseCore 0:
  22.7 43.7 all-gather.8
  69.0 32.6 all-gather.10
  119.3 41.5 reduce-scatter.9
  163.2 44.4 all-gather.14
  209.8 43.4 all-gather.12
  255.3 42.3 all-gather.18
  299.5 31.0 all-gather.16
  344.6 41.5 reduce-scatter.13
  390.1 42.6 all-gather.20
  436.0 44.8 reduce-scatter.21
  484.3 46.0 reduce-scatter.23
  533.7 46.0 reduce-scatter.25
  583.0 36.6 reduce-scatter.19
  622.9 42.3 reduce-scatter.17
  667.5 41.5 reduce-scatter.15
  711.3 41.7 reduce-scatter.11
where the time goes:
time: 771 us; the launch traced here: 764 us
  waiting for transfers between devices  557 us (72%)
  matrix products  86.6 us (11%)
  blocking collectives  52.9 us (7%)
  other arithmetic  28.6 us (4%)
  local copies, waits for them, and re-layouts  22.7 us (3%)
  between operations  14.8 us (2%)
    reduce_scatter x5, waiting for transfers between devices, reduce_weights(): lax.psum_scatter(low, 'dp', scatter_dimension=0, tiled=True)  181 us
    all_gather x4, waiting for transfers between devices, gather_rows(): return lax.all_gather(rows, 'tensor', axis=1, tiled=True)  142 us
    reduce_scatter x4, waiting for transfers between devices, scatter_rows(): lax.psum_scatter(low, 'tensor', scatter_dimension=1, tiled=True)  123 us
    psum x1, blocking collectives, local(): lax.psum(jnp.stack([term_gain1, term_gain2], axis=0), ('dp', 'tensor'))  42.5 us
    all_gather x1, waiting for transfers between devices, gather_weights(): lax.all_gather(jnp.concatenate([w_gate, w_up], axis=1), 'dp', axis=0, til...  41.2 us
    all_gather x1, waiting for transfers between devices, gather_weights(): lax.all_gather(jnp.concatenate([w_query, w_key, w_value, w_out.T], axis=1...  35.2 us
    all_gather x1, waiting for transfers between devices, gather_weights(): down = lax.all_gather(w_down.T, 'dp', axis=0, tiled=True)  32.9 us
    dot_general x5, matrix products, contract_rows(): lax.dot_general(left, right, (((0,), (0,)), ((), ())), preferred_element_...  24.8 us
  transfers between devices with their start and end apart: 16, of which 15 were waited for; matrix products, arithmetic and copies ran while one was open for 12% of the time, Pallas kernels for 0%

commit v1 on v0

--- a/solution.py
+++ b/solution.py
@@ -2,6 +2,7 @@
 import jax.numpy as jnp
 from jax import lax
 from jax.sharding import PartitionSpec as P
+from jax.lax import all_gather
 
 HEAD = 96
 eps = 1e-05
@@ -199,7 +200,8 @@
     final_in = reduce_weights(contract_rows(flat1, grad_in))
     term_gain1 = jnp.sum(grad_norm1 * unit1, axis=(0, 1))
     grad_tokens = grad_resid + norm_backward(grad_norm1, unit1, scale1, gain1)
-    gain_terms = lax.psum(jnp.stack([term_gain1, term_gain2], axis=0), ("dp", "tensor"))
+    block_here = jnp.stack([term_gain1, term_gain2], axis=0)
+    gain_terms = all_gather(block_here, ("dp", "tensor")).sum(axis=0)
     own = gain_attn.shape[0]
     gain_own = lax.dynamic_slice_in_dim(gain_terms, lax.axis_index("dp") * own, own, 1)
     return (

time: 771 us -> 802 us (1.040)
  blocking collectives: 52.9 us -> 83.9 us
    all_gather x0 -> x1, blocking collectives: none -> 73.5 us  [local(): gain_terms = all_gather(block_here, ('dp', 'tensor')).sum(axis=0)]
    psum x1 -> x0, blocking collectives: 42.5 us -> none  [local(): lax.psum(jnp.stack([term_gain1, term_gain2], axis=0), ('dp', 'tensor'))]
  transfers between devices with their start and end apart: 16 -> 16, of which waited for: 15 -> 15; matrix products, arithmetic and copies ran while one was open for 12% -> 11% of each run, Pallas kernels for 0% -> 0%
where the time goes in v1:
time: 802 us; the launch traced here: 795 us
  waiting for transfers between devices  557 us (69%)
  matrix products  86.5 us (11%)
  blocking collectives  83.9 us (10%)
  other arithmetic  28.6 us (4%)
  local copies, waits for them, and re-layouts  22.7 us (3%)
  between operations  14.8 us (2%)
    reduce_scatter x5, waiting for transfers between devices, reduce_weights(): lax.psum_scatter(low, 'dp', scatter_dimension=0, tiled=True)  181 us
    all_gather x4, waiting for transfers between devices, gather_rows(): return lax.all_gather(rows, 'tensor', axis=1, tiled=True)  142 us
    reduce_scatter x4, waiting for transfers between devices, scatter_rows(): lax.psum_scatter(low, 'tensor', scatter_dimension=1, tiled=True)  123 us
    all_gather x1, blocking collectives, local(): gain_terms = all_gather(block_here, ('dp', 'tensor')).sum(axis=0)  73.5 us
    all_gather x1, waiting for transfers between devices, gather_weights(): lax.all_gather(jnp.concatenate([w_gate, w_up], axis=1), 'dp', axis=0, til...  41.2 us
    all_gather x1, waiting for transfers between devices, gather_weights(): lax.all_gather(jnp.concatenate([w_query, w_key, w_value, w_out.T], axis=1...  35.2 us
    all_gather x1, waiting for transfers between devices, gather_weights(): down = lax.all_gather(w_down.T, 'dp', axis=0, tiled=True)  32.9 us
    dot_general x5, matrix products, contract_rows(): lax.dot_general(left, right, (((0,), (0,)), ((), ())), preferred_element_...  24.8 us
  transfers between devices with their start and end apart: 16, of which 15 were waited for; matrix products, arithmetic and copies ran while one was open for 11% of the time, Pallas kernels for 0%

profile of v1, /device:TPU:0, one launch (start us, length us, event | category | flops | bytes accessed | tf_op | source)
XLA Modules:
  0.0 794.7 jit_solution(8344042941608497038)
XLA Ops:
  7.3 0.8 stack.18
  8.8 1.2 fusion.38
  10.0 10.4 %all-gather.1 = bf16[8,192,2]{1,2,0:T(2,128)(2,1)S(1)} all-gather(bf16[1,192,2]{1,2,0:T(2,128)(2,1)S(1)} %maximum_bitcast_fusion.9), channel_id=1, replica_groups=mesh['dp'=8,'tensor'=4] {'dp'}, dimensions={0}, use_global_device_ids=true | all-gather | bytes 6912 | tf_op jit(solution)/shard_map/all_gather | solution.py:65
  20.6 2.0 fusion.35
  22.7 0.9 concatenate.32
  24.2 1.0 compare_and_fusion
  25.8 40.8 %all-gather.11.cloned.1.call-done = bf16[2,320,1536]{2,1,0:T(8,128)(2,1)} async-done(((bf16[2,80,1536]{2,1,0:T(8,128)(2,1)}), bf16[2,320,1536]{2,1,0:T(8,128)(2,1)}) %all-gather.11.cloned.1.call-update) | async-done | bytes 1966096 | tf_op jit(solution)/shard_map/all_gather | solution.py:75
  66.5 35.2 %all-gather.13.cloned.1.call-done = bf16[1536,1152]{1,0:T(8,128)(2,1)} async-done(((bf16[192,1152]{1,0:T(8,128)(2,1)}), bf16[1536,1152]{1,0:T(8,128)(2,1)}) %all-gather.13.cloned.1.call-update) | async-done | bytes 3538960 | tf_op jit(solution)/shard_map/all_gather | solution.py:66
  101.7 3.9 fusion.8
  105.9 0.9 copy.89
  107.7 4.7 fusion.63
  112.5 2.7 convolution_convert_fusion.9
  115.3 3.9 convolution_convert_fusion.7
  119.2 0.9 pad_maximum_fusion
  120.3 40.7 %reduce-scatter.10.cloned.1.call-done = bf16[2,80,1536]{2,1,0:T(8,128)(2,1)} async-done(((bf16[2,320,1536]{2,1,0:T(8,128)(2,1)}), bf16[2,80,1536]{2,1,0:T(8,128)(2,1)}) %reduce-scatter.10.cloned.1.call-update) | async-done | bytes 491536 | tf_op jit(solution)/shard_map/reduce_scatter | solution.py:80
  160.9 1.3 multiply_reduce_fusion
  162.2 2.0 multiply_convert_fusion.4
  164.4 0.9 fusion.39
  166.6 41.2 %all-gather.17.cloned.1.call-done = bf16[1536,2048]{1,0:T(8,128)(2,1)} async-done(((bf16[192,2048]{1,0:T(8,128)(2,1)}), bf16[1536,2048]{1,0:T(8,128)(2,1)}) %all-gather.17.cloned.1.call-update) | async-done | bytes 6291472 | tf_op jit(solution)/shard_map/all_gather | solution.py:69
  207.8 45.5 %all-gather.15.cloned.1.call-done = bf16[2,320,1536]{2,1,0:T(8,128)(2,1)} async-done(((bf16[2,80,1536]{2,1,0:T(8,128)(2,1)}), bf16[2,320,1536]{2,1,0:T(8,128)(2,1)}) %all-gather.15.cloned.1.call-update) | async-done | bytes 1966096 | tf_op jit(solution)/shard_map/all_gather | solution.py:75
  253.3 10.0 %fusion.68 = f32[640,2048]{1,0:T(8,128)} fusion(bf16[640,1536]{1,0:T(8,128)(2,1)} %bitcast.149, bf16[1536,2048]{1,0:T(8,128)(2,1)} %all-gather.17.cloned.1.call-done), kind=kOutput, calls=%fused_computation.125 | convolution fusion | flops 4026531840 | bytes 13500416 | tf_op jit(solution)/shard_map/dot_general | solution.py:151
  263.3 34.4 %all-gather.21.cloned.1.call-done = bf16[2,320,1536]{2,1,0:T(8,128)(2,1)} async-done(((bf16[2,80,1536]{2,1,0:T(8,128)(2,1)}), bf16[2,320,1536]{2,1,0:T(8,128)(2,1)}) %all-gather.21.cloned.1.call-update) | async-done | bytes 1966096 | tf_op jit(solution)/shard_map/all_gather | solution.py:75
  297.7 32.9 %all-gather.19.cloned.1.call-done = bf16[1536,1024]{1,0:T(8,128)(2,1)} async-done(((bf16[192,1024]{1,0:T(8,128)(2,1)}), bf16[1536,1024]{1,0:T(8,128)(2,1)}) %all-gather.19.cloned.1.call-update) | async-done | bytes 3145744 | tf_op jit(solution)/shard_map/all_gather | solution.py:70
  330.6 8.4 %multiply_convert_fusion.1 = (bf16[640,1024]{1,0:T(8,128)(2,1)S(1)}, bf16[640,1024]{1,0:T(8,128)(2,1)S(1)}, bf16[640,1024]{1,0:T(8,128)(2,1)}) fusion(f32[640,2048]{1,0:T(8,128)} %fusion.68, bf16[640,1536]{1,0:T(8,128)(2,1)} %bitcast.152, bf16[1536,1024]{1,0:T(8,128)(2,1)} %all-gather.19.cloned.1.call-done), kind=kOutput, calls=%fused_computation.22 | convolution fusion | flops 2023751680 | bytes 14286848 | tf_op jit(solution)/shard_map/dot_general | solution.py:157
  339.0 5.5 convolution_convert_fusion.5
  344.6 41.7 %reduce-scatter.14.cloned.1.call-done = bf16[2,80,1536]{2,1,0:T(8,128)(2,1)} async-done(((bf16[2,320,1536]{2,1,0:T(8,128)(2,1)}), bf16[2,80,1536]{2,1,0:T(8,128)(2,1)}) %reduce-scatter.14.cloned.1.call-update) | async-done | bytes 491536 | tf_op jit(solution)/shard_map/reduce_scatter | solution.py:80
  386.3 1.5 fusion.34
  387.8 2.2 fusion.43
  390.1 6.2 convolution_convert_fusion.2
  396.5 6.4 convolution_convert_fusion.1
  403.0 6.3 convolution_convert_fusion
  410.0 1.2 convert_element_type.210
  411.2 21.6 %all-gather.23.cloned.1.call-done = bf16[2,320,1536]{2,1,0:T(8,128)(2,1)} async-done(((bf16[2,80,1536]{2,1,0:T(8,128)(2,1)}), bf16[2,320,1536]{2,1,0:T(8,128)(2,1)}) %all-gather.23.cloned.1.call-update) | async-done | bytes 1966096 | tf_op jit(solution)/shard_map/all_gather | solution.py:75
  432.8 3.0 convolution_convert_fusion.10
  437.1 2.9 fusion.23
  440.3 0.9 convert_element_type.204
  441.2 3.3 fusion.1
  446.5 1.6 convolution_bitcast_fusion.1
  448.5 2.5 convolution_convert_fusion.8
  451.2 1.2 add_convert_fusion.1
  452.5 1.0 copy.100
  453.5 1.9 convert_element_type.201
  455.4 1.6 convolution_multiply_fusion
  458.5 0.9 copy-done.22
  460.3 3.4 convolution_convert_fusion.3
  463.8 1.2 copy-done.23
  464.9 4.8 convolution_convert_fusion.4
  469.8 1.2 copy-done.33
  471.0 5.4 convolution_convert_fusion.6
  476.5 4.5 reduce-scatter.22.cloned.1.call-done
  481.0 2.0 convert_element_type.213
  482.9 47.5 %reduce-scatter.24.cloned.1.call-done = bf16[192,1024]{1,0:T(8,128)(2,1)} async-done(((bf16[1536,1024]{1,0:T(8,128)(2,1)}), bf16[192,1024]{1,0:T(8,128)(2,1)}) %reduce-scatter.24.cloned.1.call-update) | async-done | bytes 393232 | tf_op jit(solution)/shard_map/reduce_scatter | solution.py:85
  530.5 2.0 convert_element_type.215
  532.4 47.4 %reduce-scatter.26.cloned.1.call-done = bf16[192,1024]{1,0:T(8,128)(2,1)} async-done(((bf16[1536,1024]{1,0:T(8,128)(2,1)}), bf16[192,1024]{1,0:T(8,128)(2,1)}) %reduce-scatter.26.cloned.1.call-update) | async-done | bytes 393232 | tf_op jit(solution)/shard_map/reduce_scatter | solution.py:85
  579.8 2.0 convert_bitcast_fusion
  581.8 38.0 %reduce-scatter.20.cloned.1.call-done = bf16[192,384]{1,0:T(8,128)(2,1)} async-done(((bf16[1536,384]{1,0:T(8,128)(2,1)}), bf16[192,384]{1,0:T(8,128)(2,1)}) %reduce-scatter.20.cloned.1.call-update) | async-done | bytes 147472 | tf_op jit(solution)/shard_map/reduce_scatter | solution.py:85
  619.7 1.6 convert_bitcast_fusion.1
  621.4 43.9 %reduce-scatter.18.cloned.1.call-done = bf16[192,768]{1,0:T(8,128)(2,1)} async-done(((bf16[1536,768]{1,0:T(8,128)(2,1)}), bf16[192,768]{1,0:T(8,128)(2,1)}) %reduce-scatter.18.cloned.1.call-update) | async-done | bytes 294928 | tf_op jit(solution)/shard_map/reduce_scatter | solution.py:85
  665.3 1.6 slice.110
  667.0 1.7 fusion.61
  668.7 40.4 %reduce-scatter.16.cloned.1.call-done = bf16[2,80,1536]{2,1,0:T(8,128)(2,1)} async-done(((bf16[2,320,1536]{2,1,0:T(8,128)(2,1)}), bf16[2,80,1536]{2,1,0:T(8,128)(2,1)}) %reduce-scatter.16.cloned.1.call-update) | async-done | bytes 491536 | tf_op jit(solution)/shard_map/reduce_scatter | solution.py:80
  709.1 1.5 fusion.37
  710.7 73.5 %all-gather.2 = f32[32,2,1536]{2,1,0:T(2,128)S(1)} all-gather(f32[1,2,1536]{2,1,0:T(2,128)S(1)} %maximum_bitcast_fusion.8), channel_id=2, replica_groups=mesh['dp'=8,'tensor'=4] {'dp','tensor'}, dimensions={0}, use_global_device_ids=true | all-gather | bytes 405504 | tf_op jit(solution)/shard_map/all_gather | solution.py:204
  785.0 3.0 fusion.30
  (146 shorter events, 13.2 us)
Async XLA Ops:
  7.2 15.5 %copy-start.25 = (bf16[384,192]{0,1:T(8,128)(2,1)S(1)}, bf16[384,192]{0,1:T(8,128)(2,1)}, u32[]{:S(2)}) copy-start(bf16[384,192]{0,1:T(8,128)(2,1)} %param.21) | copy-start | bytes 442372
  7.2 15.5 %copy-start.27 = (bf16[192,192]{1,0:T(8,128)(2,1)S(1)}, bf16[192,192]{1,0:T(8,128)(2,1)}, u32[]{:S(2)}) copy-start(bf16[192,192]{1,0:T(8,128)(2,1)} %param.20) | copy-start | bytes 221188
  7.2 15.5 %copy-start.26 = (bf16[192,192]{1,0:T(8,128)(2,1)S(1)}, bf16[192,192]{1,0:T(8,128)(2,1)}, u32[]{:S(2)}) copy-start(bf16[192,192]{1,0:T(8,128)(2,1)} %param.19) | copy-start | bytes 221188
  7.2 15.5 %copy-start.24 = (bf16[192,384]{1,0:T(8,128)(2,1)S(1)}, bf16[192,384]{1,0:T(8,128)(2,1)}, u32[]{:S(2)}) copy-start(bf16[192,384]{1,0:T(8,128)(2,1)} %param.18) | copy-start | bytes 442372
  7.2 16.4 %copy-start.29 = (s32[2,3]{1,0:T(2,128)S(1)}, s32[2,3]{1,0:T(2,128)}, u32[]{:S(2)}) copy-start(s32[2,3]{1,0:T(2,128)} %param.16) | copy-start | bytes 76
  7.2 16.8 %copy-start.28 = (s32[2,320]{1,0:T(2,128)S(1)}, s32[2,320]{1,0:T(2,128)}, u32[]{:S(2)}) copy-start(s32[2,320]{1,0:T(2,128)} %param.15) | copy-start | bytes 7684
  7.2 59.3 %all-gather.11.cloned.1.call-start = ((), (), s32[]{:S(2)}) async-start(), calls=%async_computation.9 | async-start | bytes 2457600 | tf_op jit(solution)/shard_map/all_gather | solution.py:75
  22.6 79.1 %all-gather.13.cloned.1.call-start = ((), (), s32[]{:S(2)}) async-start(), calls=%async_computation.10 | async-start | bytes 3981312 | tf_op jit(solution)/shard_map/all_gather | solution.py:66
  23.6 137.3 %reduce-scatter.10.cloned.1.call-start = ((), (), s32[]{:S(2)}) async-start(), calls=%async_computation.11 | async-start | bytes 2457600 | tf_op jit(solution)/shard_map/reduce_scatter | solution.py:80
  25.8 81.8 %copy-start.5 = (f32[2,320,48]{1,2,0:T(8,128)}, f32[2,320,48]{1,2,0:T(8,128)S(1)}, u32[]{:S(2)}) copy-start(f32[2,320,48]{1,2,0:T(8,128)S(1)} %get-tuple-element.34) | copy-start | bytes 368644
  25.8 81.8 %copy-start.7 = (f32[2,320,48]{1,2,0:T(8,128)}, f32[2,320,48]{1,2,0:T(8,128)S(1)}, u32[]{:S(2)}) copy-start(f32[2,320,48]{1,2,0:T(8,128)S(1)} %get-tuple-element.35) | copy-start | bytes 368644
  107.5 5.0 copy-start.16
  107.5 5.0 copy-start.17
  107.7 4.8 copy-start.9
  107.7 4.8 copy-start.11
  107.7 4.8 copy-start.21
  115.2 4.0 copy-start.19
  115.2 4.0 copy-start.20
  119.1 41.8 %copy-start = (bf16[2,80,1536]{2,1,0:T(8,128)(2,1)S(1)}, bf16[2,80,1536]{2,1,0:T(8,128)(2,1)}, u32[]{:S(2)}) copy-start(bf16[2,80,1536]{2,1,0:T(8,128)(2,1)} %param.13) | copy-start | bytes 1474564
  119.2 88.6 %all-gather.17.cloned.1.call-start = ((), (), s32[]{:S(2)}) async-start(), calls=%async_computation.13 | async-start | bytes 7077888 | tf_op jit(solution)/shard_map/all_gather | solution.py:69
  120.2 44.2 %copy-start.2 = (bf16[2,80,1536]{2,1,0:T(8,128)(2,1)S(1)}, bf16[2,80,1536]{2,1,0:T(8,128)(2,1)}, u32[]{:S(2)}) copy-start(bf16[2,80,1536]{2,1,0:T(8,128)(2,1)} %param.14) | copy-start | bytes 1474564
  120.2 133.1 %all-gather.15.cloned.1.call-start = ((), (), s32[]{:S(2)}) async-start(), calls=%async_computation.12 | async-start | bytes 2457600 | tf_op jit(solution)/shard_map/all_gather | solution.py:75
  164.2 133.4 %all-gather.21.cloned.1.call-start = ((), (), s32[]{:S(2)}) async-start(), calls=%async_computation.16 | async-start | bytes 2457600 | tf_op jit(solution)/shard_map/all_gather | solution.py:75
  165.3 165.3 %all-gather.19.cloned.1.call-start = ((), (), s32[]{:S(2)}) async-start(), calls=%async_computation.14 | async-start | bytes 3538944 | tf_op jit(solution)/shard_map/all_gather | solution.py:70
  166.1 220.2 %reduce-scatter.14.cloned.1.call-start = ((), (), s32[]{:S(2)}) async-start(), calls=%async_computation.17 | async-start | bytes 2457600 | tf_op jit(solution)/shard_map/reduce_scatter | solution.py:80
  330.6 8.4 %copy-start.30 = (bf16[1536,2048]{1,0:T(8,128)(2,1)S(1)}, bf16[1536,2048]{1,0:T(8,128)(2,1)}, u32[]{:S(2)}) copy-start(bf16[1536,2048]{1,0:T(8,128)(2,1)} %all-gather.17.cloned.1.call-done) | copy-start | bytes 18874372
  339.0 5.5 copy-start.34
  339.0 5.5 copy-start.35
  344.5 41.8 %copy-start.1 = (bf16[2,80,1536]{2,1,0:T(8,128)(2,1)S(1)}, bf16[2,80,1536]{2,1,0:T(8,128)(2,1)}, u32[]{:S(2)}) copy-start(bf16[2,80,1536]{2,1,0:T(8,128)(2,1)} %reduce-scatter.10.cloned.1.call-done) | copy-start | bytes 1474564
  344.5 88.3 %all-gather.23.cloned.1.call-start = ((), (), s32[]{:S(2)}) async-start(), calls=%async_computation.18 | async-start | bytes 2457600 | tf_op jit(solution)/shard_map/all_gather | solution.py:75
  390.0 90.9 %reduce-scatter.22.cloned.1.call-start = ((), (), s32[]{:S(2)}) async-start(), calls=%async_computation.22 | async-start | bytes 3538944 | tf_op jit(solution)/shard_map/reduce_scatter | solution.py:85
  396.3 134.2 %reduce-scatter.24.cloned.1.call-start = ((), (), s32[]{:S(2)}) async-start(), calls=%async_computation.23 | async-start | bytes 3538944 | tf_op jit(solution)/shard_map/reduce_scatter | solution.py:85
  402.9 176.9 %reduce-scatter.26.cloned.1.call-start = ((), (), s32[]{:S(2)}) async-start(), calls=%async_computation.24 | async-start | bytes 3538944 | tf_op jit(solution)/shard_map/reduce_scatter | solution.py:85
  409.3 210.4 %reduce-scatter.20.cloned.1.call-start = ((), (), s32[]{:S(2)}) async-start(), calls=%async_computation.21 | async-start | bytes 1327104 | tf_op jit(solution)/shard_map/reduce_scatter | solution.py:85
  441.2 3.9 copy-start.4
  445.1 1.1 copy-start.10
  445.1 1.3 copy-start.12
  446.5 1.6 copy-start.18
  446.5 2.0 copy-start.32
  451.0 214.3 %reduce-scatter.18.cloned.1.call-start = ((), (), s32[]{:S(2)}) async-start(), calls=%async_computation.20 | async-start | bytes 2654208 | tf_op jit(solution)/shard_map/reduce_scatter | solution.py:85
  455.4 1.6 copy-start.6
  455.4 1.7 copy-start.8
  457.2 1.2 copy-start.15
  457.3 1.2 copy-start.14
  458.4 1.9 copy-start.31
  458.5 0.9 copy-start.22
  463.7 1.2 copy-start.23
  463.7 245.4 %reduce-scatter.16.cloned.1.call-start = ((), (), s32[]{:S(2)}) async-start(), calls=%async_computation.19 | async-start | bytes 2457600 | tf_op jit(solution)/shard_map/reduce_scatter | solution.py:80
  469.7 1.3 copy-start.33
  469.7 315.2 %reduce-scatter.12.cloned.1.call-start = ((), (), s32[]{:S(2)}) async-start(), calls=%async_computation.15 | async-start | bytes 2457600 | tf_op jit(solution)/shard_map/reduce_scatter | solution.py:80
  581.8 203.2 %copy-start.3 = (bf16[2,80,1536]{2,1,0:T(8,128)(2,1)S(1)}, bf16[2,80,1536]{2,1,0:T(8,128)(2,1)}, u32[]{:S(2)}) copy-start(bf16[2,80,1536]{2,1,0:T(8,128)(2,1)} %reduce-scatter.14.cloned.1.call-done) | copy-start | bytes 1474564
  709.1 75.8 %copy-start.13 = (bf16[2,80,1536]{2,1,0:T(8,128)(2,1)S(1)}, bf16[2,80,1536]{2,1,0:T(8,128)(2,1)}, u32[]{:S(2)}) copy-start(bf16[2,80,1536]{2,1,0:T(8,128)(2,1)} %reduce-scatter.16.cloned.1.call-done) | copy-start | bytes 1474564
Sparse Core Ops, SparseCore 0:
  22.7 43.7 all-gather.10
  69.0 32.6 all-gather.12
  119.3 41.5 reduce-scatter.9
  163.2 44.5 all-gather.16
  209.8 43.4 all-gather.14
  255.3 42.3 all-gather.20
  299.5 31.0 all-gather.18
  344.6 41.5 reduce-scatter.13
  390.2 42.6 all-gather.22
  436.0 44.8 reduce-scatter.21
  484.4 46.0 reduce-scatter.23
  533.7 46.0 reduce-scatter.25
  583.0 36.6 reduce-scatter.19
  622.9 42.3 reduce-scatter.17
  667.5 41.5 reduce-scatter.15
  711.3 44.6 reduce-scatter.11
